TPU v7x, 32 devices: a whole 2x2x4 slice. The times are simulated.
32 devices in a mesh: ctx: 8 (over z, x), heads: 4 (over y, core).
Axes of the slice: x: 2, y: 2, z: 4, core: 2. Of those that a mesh axis runs over, the one named last changes fastest.
Arguments:
- query_rows: bfloat16 [8, 16, 2, 128], P('ctx', 'heads'), may hold values from -6 to 6
- past_keys: bfloat16 [8, 16, 512, 128], P(None, 'heads', 'ctx'), may hold values from -6 to 6
- past_values: bfloat16 [8, 16, 512, 128], P(None, 'heads', 'ctx'), may hold values from -6 to 6
- used_length: int32 [8], replicated, may hold values from 256 to 512
Outputs:
- read: bfloat16 [8, 16, 2, 128], P('ctx', 'heads')
All inputs are finite; a program needn't handle non-finite values.
Results may differ from a plain program's by a relative error of at most 0.0015.
Values may be sent and summed in bfloat16 or wider, within the bound.
A program may use at most 64 MiB of HBM per device.

v0:
```python
import jax
import jax.numpy as jnp
from jax import lax
from jax.sharding import PartitionSpec as P

HEAD_SIZE = 128


def local(query_rows, past_keys, past_values, used_length):
    all_queries = lax.all_gather(query_rows, "ctx", axis=0, tiled=True)
    logit = jnp.einsum(
        "bkgd,bktd->bkgt", all_queries, past_keys, preferred_element_type=jnp.float32
    ) * HEAD_SIZE ** (-0.5)
    positions = lax.axis_index("ctx") * past_keys.shape[2] + jnp.arange(past_keys.shape[2])
    filled = positions[None, :] < used_length[:, None]
    logit = jnp.where(filled[:, None, None, :], logit, -1e30)
    top = jnp.max(logit, axis=-1)
    part = jnp.where(filled[:, None, None, :], jnp.exp(logit - top[..., None]), 0.0)
    weight_sum = jnp.sum(part, axis=-1)
    read_sum = jnp.einsum(
        "bkgt,bktd->bkgd", part, past_values.astype(jnp.float32), precision=lax.Precision.HIGHEST
    )
    tops, sums, parts = (
        lax.all_to_all(top[None], "ctx", split_axis=1, concat_axis=0, tiled=True),
        lax.all_to_all(weight_sum[None], "ctx", split_axis=1, concat_axis=0, tiled=True),
        lax.all_to_all(read_sum[None], "ctx", split_axis=1, concat_axis=0, tiled=True),
    )
    best = jnp.max(tops, axis=0)
    scale = jnp.exp(tops - best)
    weight_own = jnp.sum(sums * scale, axis=0)
    read_own = jnp.sum(parts * scale[..., None], axis=0)
    read = (read_own / weight_own[..., None]).astype(jnp.bfloat16)
    return read


def solution(mesh):
    return jax.shard_map(
        local,
        mesh=mesh,
        in_specs=(
            P("ctx", "heads", None, None),
            P(None, "heads", "ctx", None),
            P(None, "heads", "ctx", None),
            P(),
        ),
        out_specs=P("ctx", "heads", None, None),
        check_vma=False,
    )
```

profile of v0, /device:TPU:0, one launch (start us, length us, event | category | flops | bytes accessed | tf_op | source)
XLA Modules:
  0.0 62.1 jit_solution(10074065572557208397)
XLA Ops:
  0.0 0.0 copy-start
  0.0 0.0 copy-start.1
  0.0 0.7 %copy-done.1 = bf16[1,4,2,128]{3,2,1,0:T(2,128)(2,1)S(1)} copy-done((bf16[1,4,2,128]{3,2,1,0:T(2,128)(2,1)S(1)}, bf16[1,4,2,128]{3,2,1,0:T(2,128)(2,1)}, u32[]{:S(2)}) %copy-start.1) | copy-done | bytes 2072
  0.7 0.0 copy-start.2
  0.8 28.1 %all_gather.3 = bf16[8,4,2,128]{3,1,2,0:T(4,128)(2,1)S(1)} all-gather(bf16[1,4,2,128]{3,1,2,0:T(4,128)(2,1)S(1)} %copy.7), channel_id=1, replica_groups=mesh['ctx'=8,'heads'=4] {'ctx'}, dimensions={0}, use_global_device_ids=true | all-gather | bytes 18432 | tf_op jit(solution)/shard_map/all_gather | solution.py:10
  28.8 0.0 copy-done.2
  28.8 0.1 broadcast_compare_fusion
  28.9 1.5 %fusion.10 = (f32[8,4,2]{2,1,0:T(4,128)S(1)}, f32[8,4,2,64]{3,2,1,0:T(2,128)S(1)}) fusion(bf16[8,4,64,128]{3,2,1,0:T(8,128)(2,1)} %param.5, bf16[8,4,2,128]{3,1,2,0:T(4,128)(2,1)S(1)} %all_gather.3, pred[8,64]{1,0:T(8,128)(4,1)S(1)} %broadcast_compare_fusion), kind=kOutput, calls=%fused_computation.19 | convolution fusion | flops 1060800 | bytes 557824 | tf_op jit(solution)/shard_map/bkgd,bktd->bkgt/dot_general | solution.py:11
  30.4 0.7 %copy.11 = f32[1,8,4,2]{2,3,0,1:T(2,128)} copy(f32[1,8,4,2]{3,2,1,0:T(4,128)S(1)} %bitcast.30) | data formatting | bytes 512 | tf_op jit(solution)/shard_map/broadcast_in_dim | solution.py:24
  31.1 4.0 %all-to-all-start.1 = ((f32[1,8,4,2]{2,3,0,1:T(2,128)}), f32[1,8,4,2]{2,3,0,1:T(2,128)S(1)}, u32[]{:S(2)}, u32[]{:S(2)}) async-start(f32[1,8,4,2]{2,3,0,1:T(2,128)} %copy.11), calls=%async_computation.1 | async-start | bytes 16384 | tf_op jit(solution)/shard_map/all_to_all | solution.py:24
  35.1 0.0 copy-done
  35.1 1.2 %convolution_bitcast_fusion = f32[1,8,4,2,128]{4,3,2,0,1:T(2,128)} fusion(bf16[8,4,64,128]{3,2,1,0:T(8,128)(2,1)S(1)} %copy-done, f32[8,4,2,64]{3,2,1,0:T(2,128)S(1)} %get-tuple-element.6, pred[8,64]{1,0:T(8,128)(4,1)S(1)} %broadcast_compare_fusion, f32[8,4,2]{2,1,0:T(4,128)S(1)} %get-tuple-element.5), kind=kOutput, calls=%fused_computation | convolution fusion | flops 6299648 | bytes 574208 | tf_op jit(solution)/shard_map/bkgt,bktd->bkgd/dot_general | solution.py:20
  36.3 0.2 fusion.8
  36.5 0.7 %copy.15 = f32[1,8,4,2]{2,3,0,1:T(2,128)} copy(f32[1,8,4,2]{3,2,1,0:T(4,128)S(1)} %bitcast.31) | data formatting | bytes 512 | tf_op jit(solution)/shard_map/broadcast_in_dim | solution.py:25
  37.2 4.4 %all-to-all-done.1 = f32[1,8,4,2]{2,3,0,1:T(2,128)S(1)} async-done(((f32[1,8,4,2]{2,3,0,1:T(2,128)}), f32[1,8,4,2]{2,3,0,1:T(2,128)S(1)}, u32[]{:S(2)}, u32[]{:S(2)}) %all-to-all-start.1) | async-done | bytes 288 | tf_op jit(solution)/shard_map/all_to_all | solution.py:24
  41.6 3.3 %all-to-all-start.2 = ((f32[1,8,4,2]{2,3,0,1:T(2,128)}), f32[1,8,4,2]{2,3,0,1:T(2,128)S(1)}, u32[]{:S(2)}, u32[]{:S(2)}) async-start(f32[1,8,4,2]{2,3,0,1:T(2,128)} %copy.15), calls=%async_computation.2 | async-start | bytes 16384 | tf_op jit(solution)/shard_map/all_to_all | solution.py:25
  44.9 0.1 copy.12
  45.0 0.1 fusion.6
  45.1 6.3 %all-to-all-done.2 = f32[1,8,4,2]{2,3,0,1:T(2,128)S(1)} async-done(((f32[1,8,4,2]{2,3,0,1:T(2,128)}), f32[1,8,4,2]{2,3,0,1:T(2,128)S(1)}, u32[]{:S(2)}, u32[]{:S(2)}) %all-to-all-start.2) | async-done | bytes 288 | tf_op jit(solution)/shard_map/all_to_all | solution.py:25
  51.4 3.3 %all-to-all-start = ((f32[1,8,4,2,128]{4,3,2,0,1:T(2,128)}), f32[1,8,4,2,128]{4,3,2,0,1:T(2,128)S(1)}, u32[]{:S(2)}, u32[]{:S(2)}) async-start(f32[1,8,4,2,128]{4,3,2,0,1:T(2,128)} %convolution_bitcast_fusion), calls=%async_computation | async-start | bytes 65536 | tf_op jit(solution)/shard_map/all_to_all | solution.py:26
  54.7 0.1 copy.16
  54.8 0.2 fusion.5
  55.0 0.1 copy.18
  55.1 0.1 copy.13
  55.2 6.2 %all-to-all-done = f32[1,8,4,2,128]{4,3,2,0,1:T(2,128)S(1)} async-done(((f32[1,8,4,2,128]{4,3,2,0,1:T(2,128)}), f32[1,8,4,2,128]{4,3,2,0,1:T(2,128)S(1)}, u32[]{:S(2)}, u32[]{:S(2)}) %all-to-all-start) | async-done | bytes 32800 | tf_op jit(solution)/shard_map/all_to_all | solution.py:26
  61.4 0.1 fusion.1
  61.5 0.7 %fusion.7 = bf16[1,4,2,128]{3,2,1,0:T(2,128)(2,1)} fusion(f32[4,2,128]{2,1,0:T(2,128)S(1)} %fusion.1, f32[4,2]{1,0:T(4,128)S(1)} %copy.18), kind=kLoop, calls=%fused_computation.14 | loop fusion | flops 2048 | bytes 6176 | tf_op jit(solution)/shard_map/convert_element_type | solution.py:32
  (3 shorter events, 0.0 us)
Async XLA Ops:
  0.0 35.1 %copy-start = (bf16[8,4,64,128]{3,2,1,0:T(8,128)(2,1)S(1)}, bf16[8,4,64,128]{3,2,1,0:T(8,128)(2,1)}, u32[]{:S(2)}) copy-start(bf16[8,4,64,128]{3,2,1,0:T(8,128)(2,1)} %param.6) | copy-start | bytes 1572868
  0.0 0.7 %copy-start.1 = (bf16[1,4,2,128]{3,2,1,0:T(2,128)(2,1)S(1)}, bf16[1,4,2,128]{3,2,1,0:T(2,128)(2,1)}, u32[]{:S(2)}) copy-start(bf16[1,4,2,128]{3,2,1,0:T(2,128)(2,1)} %param.4) | copy-start | bytes 6148
  0.7 28.1 %copy-start.2 = (s32[8]{0:T(128)S(1)}, s32[8]{0:T(128)}, u32[]{:S(2)}) copy-start(s32[8]{0:T(128)} %param.7) | copy-start | bytes 100
  31.1 10.5 %all-to-all-start.1 = ((f32[1,8,4,2]{2,3,0,1:T(2,128)}), f32[1,8,4,2]{2,3,0,1:T(2,128)S(1)}, u32[]{:S(2)}, u32[]{:S(2)}) async-start(f32[1,8,4,2]{2,3,0,1:T(2,128)} %copy.11), calls=%async_computation.1 | async-start | bytes 16384 | tf_op jit(solution)/shard_map/all_to_all | solution.py:24
  41.6 9.8 %all-to-all-start.2 = ((f32[1,8,4,2]{2,3,0,1:T(2,128)}), f32[1,8,4,2]{2,3,0,1:T(2,128)S(1)}, u32[]{:S(2)}, u32[]{:S(2)}) async-start(f32[1,8,4,2]{2,3,0,1:T(2,128)} %copy.15), calls=%async_computation.2 | async-start | bytes 16384 | tf_op jit(solution)/shard_map/all_to_all | solution.py:25
  51.4 10.0 %all-to-all-start = ((f32[1,8,4,2,128]{4,3,2,0,1:T(2,128)}), f32[1,8,4,2,128]{4,3,2,0,1:T(2,128)S(1)}, u32[]{:S(2)}, u32[]{:S(2)}) async-start(f32[1,8,4,2,128]{4,3,2,0,1:T(2,128)} %convolution_bitcast_fusion), calls=%async_computation | async-start | bytes 65536 | tf_op jit(solution)/shard_map/all_to_all | solution.py:26
where the time goes:
time: 62.5 us; the launch traced here: 62.1 us
  blocking collectives  28.1 us (45%)
  waiting for transfers between devices  16.8 us (27%)
  starting transfers between devices  10.6 us (17%)
  matrix products  2.71 us (4%)
  local copies, waits for them, and re-layouts  2.59 us (4%)
  other arithmetic  1.32 us (2%)
    all_gather x1, blocking collectives, local(): all_queries = lax.all_gather(query_rows, 'ctx', axis=0, tiled=True)  28.1 us
    all_to_all x1, waiting for transfers between devices, local(): lax.all_to_all(weight_sum[None], 'ctx', split_axis=1, concat_axis=0, tile...  6.27 us
    all_to_all x1, waiting for transfers between devices, local(): lax.all_to_all(read_sum[None], 'ctx', split_axis=1, concat_axis=0, tiled=...  6.17 us
    all_to_all x1, waiting for transfers between devices, local(): lax.all_to_all(top[None], 'ctx', split_axis=1, concat_axis=0, tiled=True)  4.37 us
    all_to_all x1, starting transfers between devices, local(): lax.all_to_all(top[None], 'ctx', split_axis=1, concat_axis=0, tiled=True)  3.97 us
    all_to_all x1, starting transfers between devices, local(): lax.all_to_all(read_sum[None], 'ctx', split_axis=1, concat_axis=0, tiled=...  3.33 us
    all_to_all x1, starting transfers between devices, local(): lax.all_to_all(weight_sum[None], 'ctx', split_axis=1, concat_axis=0, tile...  3.32 us
    dot_general x1, matrix products, local(): jnp.einsum('bkgd,bktd->bkgt', all_queries, past_keys, preferred_element_t...  1.51 us
  transfers between devices with their start and end apart: 3, of which 3 were waited for; matrix products, arithmetic and copies ran while one was open for 4% of the time, Pallas kernels for 0%

commit v1 on v0

--- a/solution.py
+++ b/solution.py
@@ -4,6 +4,12 @@
 from jax.sharding import PartitionSpec as P
 
 HEAD_SIZE = 128
+
+
+def stacked_exchange(block, axis, split, join):
+    pieces = jnp.split(block, lax.axis_size(axis), axis=split)
+    got = lax.all_to_all(jnp.stack(pieces), axis, 0, 0)
+    return jnp.concatenate(got, axis=join)
 
 
 def local(query_rows, past_keys, past_values, used_length):
@@ -21,7 +27,7 @@
         "bkgt,bktd->bkgd", part, past_values.astype(jnp.float32), precision=lax.Precision.HIGHEST
     )
     tops, sums, parts = (
-        lax.all_to_all(top[None], "ctx", split_axis=1, concat_axis=0, tiled=True),
+        stacked_exchange(top[None], "ctx", 1, 0),
         lax.all_to_all(weight_sum[None], "ctx", split_axis=1, concat_axis=0, tiled=True),
         lax.all_to_all(read_sum[None], "ctx", split_axis=1, concat_axis=0, tiled=True),
     )

time: 62.5 us -> 66.6 us (1.066)
  local copies, waits for them, and re-layouts: 2.59 us -> 6.7 us
    unnamed x7 -> x14, local copies, waits for them, and re-layouts: 0.75 us -> 4.72 us
    broadcast_in_dim x1 -> x0, local copies, waits for them, and re-layouts: 0.73 us -> none  [local(): top[None]]
where the time goes in v1:
time: 66.6 us; the launch traced here: 66.2 us
  blocking collectives  28.1 us (42%)
  waiting for transfers between devices  16.8 us (25%)
  starting transfers between devices  10.6 us (16%)
  local copies, waits for them, and re-layouts  6.7 us (10%)
  matrix products  2.71 us (4%)
  other arithmetic  1.32 us (2%)
    all_gather x1, blocking collectives, local(): all_queries = lax.all_gather(query_rows, 'ctx', axis=0, tiled=True)  28.1 us
    all_to_all x1, waiting for transfers between devices, local(): lax.all_to_all(weight_sum[None], 'ctx', split_axis=1, concat_axis=0, tile...  6.27 us
    all_to_all x1, waiting for transfers between devices, local(): lax.all_to_all(read_sum[None], 'ctx', split_axis=1, concat_axis=0, tiled=...  6.17 us
    unnamed x14, local copies, waits for them, and re-layouts  4.72 us
    all_to_all x1, waiting for transfers between devices, stacked_exchange(): got = lax.all_to_all(jnp.stack(pieces), axis, 0, 0)  4.36 us
    all_to_all x1, starting transfers between devices, stacked_exchange(): got = lax.all_to_all(jnp.stack(pieces), axis, 0, 0)  3.97 us
    all_to_all x1, starting transfers between devices, local(): lax.all_to_all(read_sum[None], 'ctx', split_axis=1, concat_axis=0, tiled=...  3.33 us
    all_to_all x1, starting transfers between devices, local(): lax.all_to_all(weight_sum[None], 'ctx', split_axis=1, concat_axis=0, tile...  3.32 us
  transfers between devices with their start and end apart: 3, of which 3 were waited for; matrix products, arithmetic and copies ran while one was open for 4% of the time, Pallas kernels for 0%

profile of v1, /device:TPU:0, one launch (start us, length us, event | category | flops | bytes accessed | tf_op | source)
XLA Modules:
  0.0 66.2 jit_solution(1190781156331781300)
XLA Ops:
  0.0 0.0 copy-start
  0.0 0.0 copy-start.1
  0.0 0.7 %copy-done.1 = bf16[1,4,2,128]{3,2,1,0:T(2,128)(2,1)S(1)} copy-done((bf16[1,4,2,128]{3,2,1,0:T(2,128)(2,1)S(1)}, bf16[1,4,2,128]{3,2,1,0:T(2,128)(2,1)}, u32[]{:S(2)}) %copy-start.1) | copy-done | bytes 2072
  0.7 0.0 copy-start.2
  0.8 28.1 %all_gather.3 = bf16[8,4,2,128]{3,1,2,0:T(4,128)(2,1)S(1)} all-gather(bf16[1,4,2,128]{3,1,2,0:T(4,128)(2,1)S(1)} %copy.13), channel_id=1, replica_groups=mesh['ctx'=8,'heads'=4] {'ctx'}, dimensions={0}, use_global_device_ids=true | all-gather | bytes 18432 | tf_op jit(solution)/shard_map/all_gather | solution.py:16
  28.8 0.0 copy-done.2
  28.8 0.1 broadcast_compare_fusion
  28.9 1.5 %fusion.10 = (f32[8,4,2]{2,1,0:T(4,128)S(1)}, f32[8,4,2,64]{3,2,1,0:T(2,128)S(1)}) fusion(bf16[8,4,64,128]{3,2,1,0:T(8,128)(2,1)} %param.5, bf16[8,4,2,128]{3,1,2,0:T(4,128)(2,1)S(1)} %all_gather.3, pred[8,64]{1,0:T(8,128)(4,1)S(1)} %broadcast_compare_fusion), kind=kOutput, calls=%fused_computation.35 | convolution fusion | flops 1060800 | bytes 557824 | tf_op jit(solution)/shard_map/bkgd,bktd->bkgt/dot_general | solution.py:17
  30.4 0.1 copy.16
  30.5 0.2 slice_reduce_fusion
  30.7 0.6 constant_dynamic-update-slice_fusion.7
  31.3 0.5 constant_dynamic-update-slice_fusion.6
  31.8 0.6 constant_dynamic-update-slice_fusion.5
  32.4 0.6 constant_dynamic-update-slice_fusion.4
  33.0 0.5 constant_dynamic-update-slice_fusion.3
  33.5 0.6 constant_dynamic-update-slice_fusion.2
  34.1 0.6 constant_dynamic-update-slice_fusion.1
  34.7 0.6 constant_dynamic-update-slice_fusion
  35.2 4.0 %all-to-all-start.1 = ((f32[8,1,1,4,2]{3,4,2,1,0:T(2,128)}), f32[8,1,1,4,2]{3,4,2,1,0:T(2,128)S(1)}, u32[]{:S(2)}, u32[]{:S(2)}) async-start(f32[8,1,1,4,2]{3,4,2,1,0:T(2,128)} %constant_dynamic-update-slice_fusion), calls=%async_computation.1 | async-start | bytes 16384 | tf_op jit(solution)/shard_map/all_to_all | solution.py:11
  39.2 0.0 copy-done
  39.2 1.2 %convolution_bitcast_fusion = f32[1,8,4,2,128]{4,3,2,0,1:T(2,128)} fusion(bf16[8,4,64,128]{3,2,1,0:T(8,128)(2,1)S(1)} %copy-done, f32[8,4,2,64]{3,2,1,0:T(2,128)S(1)} %get-tuple-element.14, pred[8,64]{1,0:T(8,128)(4,1)S(1)} %broadcast_compare_fusion, f32[8,4,2]{2,1,0:T(4,128)S(1)} %get-tuple-element.13), kind=kOutput, calls=%fused_computation | convolution fusion | flops 6299648 | bytes 574208 | tf_op jit(solution)/shard_map/bkgt,bktd->bkgd/dot_general | solution.py:26
  40.4 0.2 fusion.8
  40.6 0.7 %copy.20 = f32[1,8,4,2]{2,3,0,1:T(2,128)} copy(f32[1,8,4,2]{3,2,1,0:T(4,128)S(1)} %bitcast.47) | data formatting | bytes 512 | tf_op jit(solution)/shard_map/broadcast_in_dim | solution.py:31
  41.4 4.4 %all-to-all-done.1 = f32[8,1,1,4,2]{3,4,2,1,0:T(2,128)S(1)} async-done(((f32[8,1,1,4,2]{3,4,2,1,0:T(2,128)}), f32[8,1,1,4,2]{3,4,2,1,0:T(2,128)S(1)}, u32[]{:S(2)}, u32[]{:S(2)}) %all-to-all-start.1) | async-done | bytes 288 | tf_op jit(solution)/shard_map/all_to_all | solution.py:11
  45.7 3.3 %all-to-all-start.2 = ((f32[1,8,4,2]{2,3,0,1:T(2,128)}), f32[1,8,4,2]{2,3,0,1:T(2,128)S(1)}, u32[]{:S(2)}, u32[]{:S(2)}) async-start(f32[1,8,4,2]{2,3,0,1:T(2,128)} %copy.20), calls=%async_computation.2 | async-start | bytes 16384 | tf_op jit(solution)/shard_map/all_to_all | solution.py:31
  49.1 0.1 copy.17
  49.2 0.1 fusion.6
  49.2 6.3 %all-to-all-done.2 = f32[1,8,4,2]{2,3,0,1:T(2,128)S(1)} async-done(((f32[1,8,4,2]{2,3,0,1:T(2,128)}), f32[1,8,4,2]{2,3,0,1:T(2,128)S(1)}, u32[]{:S(2)}, u32[]{:S(2)}) %all-to-all-start.2) | async-done | bytes 288 | tf_op jit(solution)/shard_map/all_to_all | solution.py:31
  55.5 3.3 %all-to-all-start = ((f32[1,8,4,2,128]{4,3,2,0,1:T(2,128)}), f32[1,8,4,2,128]{4,3,2,0,1:T(2,128)S(1)}, u32[]{:S(2)}, u32[]{:S(2)}) async-start(f32[1,8,4,2,128]{4,3,2,0,1:T(2,128)} %convolution_bitcast_fusion), calls=%async_computation | async-start | bytes 65536 | tf_op jit(solution)/shard_map/all_to_all | solution.py:32
  58.9 0.1 copy.21
  58.9 0.2 fusion.5
  59.1 0.1 copy.23
  59.2 0.1 copy.18
  59.3 6.2 %all-to-all-done = f32[1,8,4,2,128]{4,3,2,0,1:T(2,128)S(1)} async-done(((f32[1,8,4,2,128]{4,3,2,0,1:T(2,128)}), f32[1,8,4,2,128]{4,3,2,0,1:T(2,128)S(1)}, u32[]{:S(2)}, u32[]{:S(2)}) %all-to-all-start) | async-done | bytes 32800 | tf_op jit(solution)/shard_map/all_to_all | solution.py:32
  65.5 0.1 fusion.1
  65.6 0.7 fusion.7
  (3 shorter events, 0.0 us)
Async XLA Ops:
  0.0 39.2 %copy-start = (bf16[8,4,64,128]{3,2,1,0:T(8,128)(2,1)S(1)}, bf16[8,4,64,128]{3,2,1,0:T(8,128)(2,1)}, u32[]{:S(2)}) copy-start(bf16[8,4,64,128]{3,2,1,0:T(8,128)(2,1)} %param.6) | copy-start | bytes 1572868
  0.0 0.7 %copy-start.1 = (bf16[1,4,2,128]{3,2,1,0:T(2,128)(2,1)S(1)}, bf16[1,4,2,128]{3,2,1,0:T(2,128)(2,1)}, u32[]{:S(2)}) copy-start(bf16[1,4,2,128]{3,2,1,0:T(2,128)(2,1)} %param.4) | copy-start | bytes 6148
  0.7 28.1 %copy-start.2 = (s32[8]{0:T(128)S(1)}, s32[8]{0:T(128)}, u32[]{:S(2)}) copy-start(s32[8]{0:T(128)} %param.7) | copy-start | bytes 100
  35.2 10.5 %all-to-all-start.1 = ((f32[8,1,1,4,2]{3,4,2,1,0:T(2,128)}), f32[8,1,1,4,2]{3,4,2,1,0:T(2,128)S(1)}, u32[]{:S(2)}, u32[]{:S(2)}) async-start(f32[8,1,1,4,2]{3,4,2,1,0:T(2,128)} %constant_dynamic-update-slice_fusion), calls=%async_computation.1 | async-start | bytes 16384 | tf_op jit(solution)/shard_map/all_to_all | solution.py:11
  45.7 9.8 %all-to-all-start.2 = ((f32[1,8,4,2]{2,3,0,1:T(2,128)}), f32[1,8,4,2]{2,3,0,1:T(2,128)S(1)}, u32[]{:S(2)}, u32[]{:S(2)}) async-start(f32[1,8,4,2]{2,3,0,1:T(2,128)} %copy.20), calls=%async_computation.2 | async-start | bytes 16384 | tf_op jit(solution)/shard_map/all_to_all | solution.py:31
  55.5 10.0 %all-to-all-start = ((f32[1,8,4,2,128]{4,3,2,0,1:T(2,128)}), f32[1,8,4,2,128]{4,3,2,0,1:T(2,128)S(1)}, u32[]{:S(2)}, u32[]{:S(2)}) async-start(f32[1,8,4,2,128]{4,3,2,0,1:T(2,128)} %convolution_bitcast_fusion), calls=%async_computation | async-start | bytes 65536 | tf_op jit(solution)/shard_map/all_to_all | solution.py:32
